TPU v7x, 32 devices: a whole 2x2x4 slice. The times are simulated.
32 devices in a mesh: rep: 16 (over z, y, core), grp: 2 (over x).
Axes of the slice: x: 2, y: 2, z: 4, core: 2. Of those that a mesh axis runs over, the one named last changes fastest.
Arguments:
- local_params: bfloat16 [16, 2, 32, 8192], P('rep', 'grp'), may hold values from -130 to 130
- snapshot: bfloat16 [2, 32, 8192], P('grp'), may hold values from -4 to 4
- master: float32 [2, 32, 8192], P('grp', 'rep'), may hold values from -6 to 6
- momentum: float32 [2, 32, 8192], P('grp', 'rep'), may hold values from -4 to 4
Outputs:
- new_master: float32 [2, 32, 8192], P('grp', 'rep')
- new_momentum: float32 [2, 32, 8192], P('grp', 'rep')
- new_params: bfloat16 [2, 32, 8192], P('grp')
All inputs are finite; a program needn't handle non-finite values.
Results may differ from a plain program's by a relative error of at most 0.001.
Values may be sent and summed in bfloat16 or wider, within the bound.
A program may use at most 128 MiB of HBM per device.

v0:
```python
import jax
import jax.numpy as jnp
from jax import lax
from jax.sharding import PartitionSpec as P

nesterov_mu = 0.9
outer_rate = 0.7
clip_limit = 0.15
epsilon = 1e-06


def body(local_params, snapshot, master, momentum):
    replicas = lax.axis_size("rep")
    own_rows = master.shape[1]
    replica_sum = jnp.sum(
        lax.all_to_all(local_params[0], "rep", split_axis=1, concat_axis=0, tiled=True).astype(
            jnp.float32
        ),
        axis=0,
        keepdims=True,
    )
    owned_snap = lax.dynamic_slice_in_dim(
        snapshot, lax.axis_index("rep") * own_rows, own_rows, 1
    ).astype(jnp.float32)
    outer_grad = owned_snap - replica_sum / replicas
    elements = snapshot.shape[1] * snapshot.shape[2] * lax.axis_size("grp")
    squares = lax.psum(jnp.sum(outer_grad * outer_grad), ("rep", "grp"))
    grad_rms = jnp.sqrt(squares / elements + epsilon)
    clipped = jnp.minimum(1.0, clip_limit / grad_rms) * outer_grad
    new_momentum = nesterov_mu * momentum + clipped
    new_master = master - outer_rate * (clipped + nesterov_mu * new_momentum)
    new_params = lax.all_gather(new_master.astype(jnp.bfloat16), "rep", axis=1, tiled=True)
    return (new_master, new_momentum, new_params)


def solution(mesh):
    return jax.shard_map(
        body,
        mesh=mesh,
        in_specs=(
            P("rep", "grp", None, None),
            P("grp", None, None),
            P("grp", "rep", None),
            P("grp", "rep", None),
        ),
        out_specs=(P("grp", "rep", None), P("grp", "rep", None), P("grp", None, None)),
        check_vma=False,
    )
```

profile of v0, /device:TPU:0, one launch (start us, length us, event | category | flops | bytes accessed | tf_op | source)
XLA Modules:
  0.0 102.9 jit_solution(10499969501519827075)
XLA Ops:
  0.6 0.0 copy-start
  0.6 2.2 %copy.40 = bf16[1,32,8192]{2,0,1:T(2,128)(2,1)S(1)} copy(bf16[1,32,8192]{2,1,0:T(8,128)(2,1)} %bitcast.7) | data formatting | bytes 1048576 | tf_op jit(solution)/shard_map/squeeze | solution.py:16
  2.9 0.5 broadcast.18
  3.4 3.8 %reduce.2 = bf16[32,8192]{1,0:T(8,128)(2,1)S(1)} reduce(bf16[32,1,8192]{2,1,0:T(2,128)(2,1)S(1)} %bitcast.6, bf16[]{:T(256)} %broadcast.18), dimensions={1}, to_apply=%bitcast.5.reduce_sub_computation | reduce | bytes 1048578
  7.2 1.1 %reshape.23 = bf16[16,2,8192]{2,1,0:T(2,128)(2,1)} reshape(bf16[32,8192]{1,0:T(8,128)(2,1)S(1)} %reduce.2) | data formatting | bytes 1048576
  8.3 7.4 %all-to-all-start = ((bf16[16,2,8192]{2,1,0:T(2,128)(2,1)}), bf16[16,2,8192]{2,1,0:T(2,128)(2,1)S(1)}, u32[]{:S(2)}, u32[]{:S(2)}) async-start(bf16[16,2,8192]{2,1,0:T(2,128)(2,1)} %reshape.23), calls=%async_computation | async-start | bytes 1048576 | tf_op jit(solution)/shard_map/all_to_all | solution.py:16
  15.7 0.0 copy-done
  15.8 14.2 %all-to-all-done = bf16[16,2,8192]{2,1,0:T(2,128)(2,1)S(1)} async-done(((bf16[16,2,8192]{2,1,0:T(2,128)(2,1)}), bf16[16,2,8192]{2,1,0:T(2,128)(2,1)S(1)}, u32[]{:S(2)}, u32[]{:S(2)}) %all-to-all-start) | async-done | bytes 524320 | tf_op jit(solution)/shard_map/all_to_all | solution.py:16
  30.0 0.5 reshape.24
  30.5 3.0 %convert_reduce_fusion = f32[32,8192]{1,0:T(8,128)S(1)} fusion(bf16[32,1,8192]{2,1,0:T(2,128)(2,1)S(1)} %reshape.24), kind=kLoop, calls=%fused_computation | loop fusion | flops 262144 | bytes 1572864 | tf_op jit(solution)/shard_map/convert_element_type | solution.py:16
  33.6 0.6 reshape.21
  34.2 0.4 reduce_sum.18
  34.6 0.0 copy-start.1
  34.6 0.7 multiply_reduce_fusion
  35.4 0.1 copy-done.1
  35.5 0.0 copy-start.2
  35.5 39.8 %psum.7 = f32[]{:T(128)} all-reduce(f32[]{:T(128)} %multiply_reduce_fusion), channel_id=1, replica_groups=mesh['rep'=16,'grp'=2] {'rep','grp'}, use_global_device_ids=true, to_apply=%region_2.0 | all-reduce | flops 1 | bytes 8 | tf_op jit(solution)/shard_map/psum | solution.py:27
  76.0 0.0 copy-done.2
  76.0 0.2 fusion.1
  76.3 0.7 copy.19
  76.9 0.7 copy.20
  77.6 23.9 %all_gather.3 = bf16[1,32,8192]{2,0,1:T(2,128)(2,1)S(1)} all-gather(bf16[1,2,8192]{2,0,1:T(2,128)(2,1)S(1)} %get-tuple-element.9), channel_id=1, replica_groups=mesh['rep'=16,'grp'=2] {'rep'}, dimensions={1}, use_global_device_ids=true | all-gather | bytes 557056 | tf_op jit(solution)/shard_map/all_gather | solution.py:32
  101.5 1.4 %copy.21 = bf16[1,32,8192]{2,1,0:T(8,128)(2,1)} copy(bf16[1,32,8192]{2,0,1:T(2,128)(2,1)S(1)} %all_gather.3) | data formatting | bytes 1048576
  (3 shorter events, 0.1 us)
Async XLA Ops:
  0.6 15.1 %copy-start = (bf16[1,32,8192]{2,1,0:T(8,128)(2,1)S(1)}, bf16[1,32,8192]{2,1,0:T(8,128)(2,1)}, u32[]{:S(2)}) copy-start(bf16[1,32,8192]{2,1,0:T(8,128)(2,1)} %param.5) | copy-start | bytes 1572868
  8.3 21.7 %all-to-all-start = ((bf16[16,2,8192]{2,1,0:T(2,128)(2,1)}), bf16[16,2,8192]{2,1,0:T(2,128)(2,1)S(1)}, u32[]{:S(2)}, u32[]{:S(2)}) async-start(bf16[16,2,8192]{2,1,0:T(2,128)(2,1)} %reshape.23), calls=%async_computation | async-start | bytes 1048576 | tf_op jit(solution)/shard_map/all_to_all | solution.py:16
  34.6 0.8 copy-start.1
  35.5 40.5 %copy-start.2 = (f32[1,2,8192]{2,1,0:T(2,128)S(1)}, f32[1,2,8192]{2,1,0:T(2,128)}, u32[]{:S(2)}) copy-start(f32[1,2,8192]{2,1,0:T(2,128)} %param.6) | copy-start | bytes 196612
where the time goes:
time: 103 us
  blocking collectives  63.7 us (62%)
  waiting for transfers between devices  14.2 us (14%)
  other arithmetic  8.25 us (8%)
  local copies, waits for them, and re-layouts  7.88 us (8%)
  starting transfers between devices  7.41 us (7%)
  between operations  1.45 us (1%)
    psum x1, blocking collectives, body(): squares = lax.psum(jnp.sum(outer_grad * outer_grad), ('rep', 'grp'))  39.8 us
    all_gather x1, blocking collectives, body(): lax.all_gather(new_master.astype(jnp.bfloat16), 'rep', axis=1, tiled=True)  23.9 us
    all_to_all x1, waiting for transfers between devices, body(): lax.all_to_all(local_params[0], 'rep', split_axis=1, concat_axis=0, tiled...  14.2 us
    all_to_all x1, starting transfers between devices, body(): lax.all_to_all(local_params[0], 'rep', split_axis=1, concat_axis=0, tiled...  7.41 us
    unnamed x12, local copies, waits for them, and re-layouts  5.01 us
    unnamed x1, other arithmetic  3.81 us
    convert_element_type x1, other arithmetic, body(): lax.all_to_all(local_params[0], 'rep', split_axis=1, concat_axis=0, tiled...  3.02 us
    squeeze x1, local copies, waits for them, and re-layouts, body(): local_params[0]  2.2 us
  transfers between devices with their start and end apart: 1, of which 1 were waited for; matrix products, arithmetic and copies ran while one was open for 0% of the time, Pallas kernels for 0%

commit v1 on v0

v1 whole, which is shorter than its diff:
```python
import functools

import jax
import jax.numpy as jnp
from jax import lax
from jax.experimental import pallas as pl
from jax.experimental.pallas import tpu as pltpu
from jax.sharding import PartitionSpec as P

nesterov_mu = 0.9
outer_rate = 0.7
clip_limit = 0.15
epsilon = 1e-06

f32 = jnp.float32
bf16 = jnp.bfloat16


def kernel(
    n, groups, own, width, elements,
    local_hbm, snap_hbm, master_hbm, mom_hbm,
    master_out, mom_out, params_out,
    local_v, snap_v, send_v, snap_own, recv_v, acc, grad, master_v, mom_v, gather_v, sq,
    in_sem, rs_send, rs_recv, sq_send, sq_recv, ag_send, ag_recv,
):
    me = lax.axis_index("rep")
    grp = lax.axis_index("grp")
    planes = n // 4
    plane = me // 4
    lane = me % 4
    total = n * groups
    my_id = grp * n + me

    loads = [pltpu.make_async_copy(local_hbm.at[p], local_v.at[p], in_sem.at[p]) for p in range(planes)]
    for c in loads:
        c.start()
    snap_load = pltpu.make_async_copy(snap_hbm.at[plane], snap_v, in_sem.at[planes])
    master_load = pltpu.make_async_copy(master_hbm.at[0], master_v, in_sem.at[planes + 1])
    mom_load = pltpu.make_async_copy(mom_hbm.at[0], mom_v, in_sem.at[planes + 2])
    snap_load.start()
    master_load.start()
    mom_load.start()

    def device(index):
        other = (my_id + index) % total
        return {"rep": other % n, "grp": other // n}

    barrier = pltpu.get_barrier_semaphore()

    @pl.loop(1, total)
    def _(i):
        pl.semaphore_signal(barrier, inc=1, device_id=device(i), device_id_type=pl.DeviceIdType.MESH)

    for p in range(planes):
        loads[p].wait()
        for j in range(4):
            send_v[p * 4 + j] = local_v[p, j * own:(j + 1) * own, :]

    pl.semaphore_wait(barrier, total - 1)

    def scatter(target, source):
        return pltpu.make_async_remote_copy(
            src_ref=send_v.at[target], dst_ref=recv_v.at[source],
            send_sem=rs_send.at[target], recv_sem=rs_recv.at[source],
            device_id={"rep": target, "grp": grp}, device_id_type=pl.DeviceIdType.MESH,
        )

    def offset(k):
        return n // 2 + (1 - 2 * (k % 2)) * ((k + 1) // 2)

    @pl.loop(0, n - 1)
    def _(k):
        scatter((me + offset(k)) % n, me).start()

    snap_load.wait()
    for j in range(4):
        snap_own[j] = snap_v[j * own:(j + 1) * own, :]
    acc[...] = send_v[me].astype(f32)
    master_load.wait()
    mom_load.wait()

    @pl.loop(0, n - 1)
    def _(k):
        source = (me + 2 * n - 1 - k) % n
        pltpu.make_async_remote_copy(
            src_ref=send_v.at[source], dst_ref=recv_v.at[source],
            send_sem=rs_send.at[source], recv_sem=rs_recv.at[source],
            device_id={"rep": source, "grp": grp}, device_id_type=pl.DeviceIdType.MESH,
        ).wait_recv()
        acc[...] += recv_v[source].astype(f32)

    grad[...] = snap_own[lane].astype(f32) - acc[...] * (1.0 / n)
    g2 = grad[...] * grad[...]
    part = g2[:, 0:128]
    for k in range(1, width // 128):
        part = part + g2[:, k * 128:(k + 1) * 128]
    sq[my_id] = jnp.sum(part, axis=0, keepdims=True)

    def share(index):
        slot = (my_id + index) % total
        return pltpu.make_async_remote_copy(
            src_ref=sq.at[my_id], dst_ref=sq.at[my_id],
            send_sem=sq_send.at[slot], recv_sem=sq_recv.at[my_id],
            device_id=device(index), device_id_type=pl.DeviceIdType.MESH,
        )

    @pl.loop(1, total)
    def _(i):
        share(i).start()

    @pl.loop(0, n - 1)
    def _(k):
        scatter((me + 1 + k) % n, me).wait_send()

    @pl.loop(1, total)
    def _(i):
        slot = (my_id + i) % total
        pltpu.make_async_remote_copy(
            src_ref=sq.at[my_id], dst_ref=sq.at[slot],
            send_sem=sq_send.at[slot], recv_sem=sq_recv.at[slot],
            device_id=device(i), device_id_type=pl.DeviceIdType.MESH,
        ).wait_recv()

    squares = jnp.sum(jnp.sum(sq[...], axis=0), axis=1, keepdims=True)
    grad_rms = jnp.sqrt(squares / elements + epsilon)
    scale = jnp.minimum(1.0, clip_limit / grad_rms)
    clipped = scale * grad[...]
    new_momentum = nesterov_mu * mom_v[...] + clipped
    new_master = master_v[...] - outer_rate * (clipped + nesterov_mu * new_momentum)
    gather_v[me] = new_master.astype(bf16)
    master_out[0] = new_master
    mom_out[0] = new_momentum

    row = lane // 2
    core = lane % 2
    twin_row = plane * 4 + (1 - row) * 2 + core
    twin_core = plane * 4 + row * 2 + 1 - core

    def move(block, target, slot):
        return pltpu.make_async_remote_copy(
            src_ref=gather_v.at[block], dst_ref=gather_v.at[block],
            send_sem=ag_send.at[slot], recv_sem=ag_recv.at[block],
            device_id={"rep": target, "grp": grp}, device_id_type=pl.DeviceIdType.MESH,
        )

    def block_of(i, r, c):
        return ((plane + i) % planes) * 4 + r * 2 + c

    for i in range(1, planes):
        move(me, block_of(i, row, core), i).start()
    move(me, twin_row, planes).start()
    move(me, twin_core, 2 * planes).start()
    for i in range(1, planes):
        block = block_of(i, row, core)
        move(block, block, 0).wait_recv()
        move(block, twin_row, planes + i).start()
        move(block, twin_core, 2 * planes + i).start()
    for i in range(planes):
        block = block_of(i, 1 - row, core)
        move(block, block, 0).wait_recv()
        move(block, twin_core, 3 * planes + i).start()
    for i in range(planes):
        for r in (row, 1 - row):
            block = block_of(i, r, 1 - core)
            move(block, block, 0).wait_recv()
        where = (plane + i) % planes
        for j in range(4):
            params_out[where, j * own:(j + 1) * own, :] = gather_v[where * 4 + j]

    @pl.loop(1, n)
    def _(k):
        move(me, twin_core, k).wait_send()

    @pl.loop(1, total)
    def _(i):
        share(i).wait_send()


def solution(mesh):
    n, groups = mesh.shape["rep"], mesh.shape["grp"]

    def body(local_params, snapshot, master, momentum):
        own, width = master.shape[1], master.shape[2]
        planes = n // 4
        span = 4 * own
        any_spec = pl.BlockSpec(memory_space=pl.ANY)
        vmem_spec = pl.BlockSpec(memory_space=pltpu.VMEM)
        new_master, new_momentum, new_params = pl.pallas_call(
            functools.partial(kernel, n, groups, own, width, snapshot.shape[1] * width * groups),
            out_shape=(
                jax.ShapeDtypeStruct(master.shape, f32),
                jax.ShapeDtypeStruct(master.shape, f32),
                jax.ShapeDtypeStruct((planes, span, width), bf16),
            ),
            in_specs=[any_spec] * 4,
            out_specs=(vmem_spec,) * 3,
            scratch_shapes=[
                pltpu.VMEM((planes, span, width), bf16),
                pltpu.VMEM((span, width), bf16),
                pltpu.VMEM((n, own, width), bf16),
                pltpu.VMEM((4, own, width), bf16),
                pltpu.VMEM((n, own, width), bf16),
                pltpu.VMEM((own, width), f32),
                pltpu.VMEM((own, width), f32),
                pltpu.VMEM((own, width), f32),
                pltpu.VMEM((own, width), f32),
                pltpu.VMEM((n, own, width), bf16),
                pltpu.VMEM((n * groups, 1, 128), f32),
                pltpu.SemaphoreType.DMA((planes + 3,)),
                pltpu.SemaphoreType.DMA((n,)),
                pltpu.SemaphoreType.DMA((n,)),
                pltpu.SemaphoreType.DMA((n * groups,)),
                pltpu.SemaphoreType.DMA((n * groups,)),
                pltpu.SemaphoreType.DMA((n,)),
                pltpu.SemaphoreType.DMA((n,)),
            ],
            compiler_params=pltpu.CompilerParams(collective_id=0, has_side_effects=True),
        )(
            local_params.reshape(planes, span, width),
            snapshot.reshape(planes, span, width),
            master,
            momentum,
        )
        return new_master, new_momentum, new_params.reshape(snapshot.shape)

    return jax.shard_map(
        body,
        mesh=mesh,
        in_specs=(
            P("rep", "grp", None, None),
            P("grp", None, None),
            P("grp", "rep", None),
            P("grp", "rep", None),
        ),
        out_specs=(P("grp", "rep", None), P("grp", "rep", None), P("grp", None, None)),
        check_vma=False,
    )
```

time: 103 us -> 39.7 us (0.39)
  blocking collectives: 63.7 us -> 0 us
  Pallas kernels: 0 us -> 34.6 us
  waiting for transfers between devices: 14.2 us -> 0 us
  other arithmetic: 8.25 us -> 0 us
  starting transfers between devices: 7.41 us -> 0 us
  local copies, waits for them, and re-layouts: 7.88 us -> 4.01 us
    psum x1 -> x0, blocking collectives: 39.8 us -> none  [body(): squares = lax.psum(jnp.sum(outer_grad * outer_grad), ('rep', 'grp'))]
    pallas_call x0 -> x1, Pallas kernels: none -> 34.6 us  [body(): pl.pallas_call(functools.partial(kernel, n, groups, own, width, snapshot....]
    all_gather x1 -> x0, blocking collectives: 23.9 us -> none  [body(): lax.all_gather(new_master.astype(jnp.bfloat16), 'rep', axis=1, tiled=True)]
    all_to_all x1 -> x0, waiting for transfers between devices: 14.2 us -> none  [body(): lax.all_to_all(local_params[0], 'rep', split_axis=1, concat_axis=0, tiled...]
    all_to_all x1 -> x0, starting transfers between devices: 7.41 us -> none  [body(): lax.all_to_all(local_params[0], 'rep', split_axis=1, concat_axis=0, tiled...]
    unnamed x1 -> x0, other arithmetic: 3.81 us -> none
    convert_element_type x2 -> x0, other arithmetic: 3.26 us -> none  [the longest x1 3.02 us: body(): lax.all_to_all(local_params[0], 'rep', split_axis=1, concat_axis=0, tiled...]
    squeeze x1 -> x0, local copies, waits for them, and re-layouts: 2.2 us -> none  [body(): local_params[0]]
  transfers between devices with their start and end apart: 1 -> 0, of which waited for: 1 -> 0; matrix products, arithmetic and copies ran while one was open for 0% -> 0% of each run, Pallas kernels for 0% -> 0%
where the time goes in v1:
time: 39.7 us; the launch traced here: 39.3 us
  Pallas kernels  34.6 us (87%)
  local copies, waits for them, and re-layouts  4.01 us (10%)
  between operations  0.65 us (2%)
    pallas_call x1, Pallas kernels, body(): pl.pallas_call(functools.partial(kernel, n, groups, own, width, snapshot....  34.6 us
    unnamed x5, local copies, waits for them, and re-layouts  4.01 us

profile of v1, /device:TPU:0, one launch (start us, length us, event | category | flops | bytes accessed | tf_op | source)
XLA Modules:
  0.0 39.3 jit_solution(4557545997160305475)
XLA Ops:
  0.6 34.6 %shard_map.67 = (f32[1,2,8192]{2,1,0:T(2,128)}, f32[1,2,8192]{2,1,0:T(2,128)}, bf16[4,8,8192]{2,1,0:T(8,128)(2,1)}) custom-call(bf16[4,8,8192]{2,1,0:T(8,128)(2,1)} %bitcast.3, bf16[4,8,8192]{2,1,0:T(8,128)(2,1)} %bitcast.4, f32[1,2,8192]{2,1,0:T(2,128)} %master_hbm.1, f32[1,2,8192]{2,1,0:T(2,128)} %mom_hbm.1), custom_call_target="tpu_custom_call" | custom-call | tf_op jit(solution)/shard_map/pallas_call | solution.py:188
  35.3 0.0 copy-start
  35.3 1.5 %copy.10 = f32[1,2,8192]{2,1,0:T(2,128)} copy(f32[1,2,8192]{2,1,0:T(2,128)} %get-tuple-element.12) | data formatting | bytes 131072
  36.8 0.0 copy-done
  36.8 0.6 %copy.11 = f32[1,2,8192]{2,1,0:T(2,128)} copy(f32[1,2,8192]{2,1,0:T(2,128)S(1)} %copy-done) | data formatting | bytes 131072
  37.4 1.9 %copy.12 = bf16[1,32,8192]{2,1,0:T(8,128)(2,1)} copy(bf16[1,32,8192]{2,1,0:T(8,128)(2,1)} %bitcast.5) | data formatting | bytes 1048576
Async XLA Ops:
  35.3 1.5 %copy-start = (f32[1,2,8192]{2,1,0:T(2,128)S(1)}, f32[1,2,8192]{2,1,0:T(2,128)}, u32[]{:S(2)}) copy-start(f32[1,2,8192]{2,1,0:T(2,128)} %get-tuple-element.13) | copy-start | bytes 196612

commit v2 on v1

v2 whole, which is shorter than its diff:
```python
import functools

import jax
import jax.numpy as jnp
from jax import lax
from jax.experimental import pallas as pl
from jax.experimental.pallas import tpu as pltpu
from jax.sharding import PartitionSpec as P

nesterov_mu = 0.9
outer_rate = 0.7
clip_limit = 0.15
epsilon = 1e-06

f32 = jnp.float32
bf16 = jnp.bfloat16


MESH = pl.DeviceIdType.MESH


def remote(src, dst, send, recv, rep, grp):
    return pltpu.make_async_remote_copy(
        src_ref=src, dst_ref=dst, send_sem=send, recv_sem=recv,
        device_id={"rep": rep, "grp": grp}, device_id_type=MESH,
    )


def each(count, body):
    if count <= 64:
        for i in range(count):
            body(i)
    else:
        pl.loop(0, count)(body)


def kernel(
    n, groups, own, fold, elements,
    local_hbm, snap_hbm, master_hbm, mom_hbm,
    master_out, mom_out, params_out,
    local_v, snap_v, master_v, mom_v, send_v, snap_own, master_d, mom_d, recv_v, gather_v, sq,
    in_sem, rs_send, rs_recv, sq_send, sq_recv, ag_send, ag_recv,
):
    me = lax.axis_index("rep")
    grp = lax.axis_index("grp")
    planes = n // 4
    plane = lax.div(me, 4)
    lane = lax.rem(me, 4)
    row = lax.div(lane, 2)
    core = lax.rem(lane, 2)
    total = n * groups
    part = send_v.shape[2]

    loads = [pltpu.make_async_copy(local_hbm.at[p], local_v.at[p], in_sem.at[p]) for p in range(planes)]
    for c in loads:
        c.start()
    snap_load = pltpu.make_async_copy(snap_hbm.at[plane], snap_v, in_sem.at[planes])
    master_load = pltpu.make_async_copy(master_hbm.at[0], master_v, in_sem.at[planes + 1])
    mom_load = pltpu.make_async_copy(mom_hbm.at[0], mom_v, in_sem.at[planes + 2])
    snap_load.start()
    master_load.start()
    mom_load.start()

    def rep_at(i):
        return lax.rem(me + i, n)

    def grp_at(i):
        return lax.rem(grp + i, groups)

    def peers(body):
        for g in range(groups):
            if g:
                body(me, grp_at(g))
            each(n - 1, lambda i, g=g: body(rep_at(n - 1 - i), grp_at(g)))

    barrier = pltpu.get_barrier_semaphore()
    peers(lambda r, g: pl.semaphore_signal(barrier, inc=1, device_id={"rep": r, "grp": g}, device_id_type=MESH))

    def rows(q):
        return slice(q * own, (q + 1) * own)

    def cols(q):
        return slice(q * part, (q + 1) * part)

    for p in range(planes):
        loads[p].wait()
        for j in range(4):
            for q in range(fold):
                send_v[p * 4 + j, rows(q), :] = local_v[p, rows(j), cols(q)]

    pl.semaphore_wait(barrier, total - 1)

    def offset(k):
        return n // 2 + (1 - 2 * (k % 2)) * ((k + 1) // 2)

    def scatter(k):
        target = rep_at(offset(k))
        remote(send_v.at[target], recv_v.at[me], rs_send.at[target], rs_recv.at[me], target, grp).start()

    each(n - 1, scatter)

    snap_load.wait()
    master_load.wait()
    mom_load.wait()
    for q in range(fold):
        for j in range(4):
            snap_own[j, rows(q), :] = snap_v[rows(j), cols(q)]
        master_d[rows(q), :] = master_v[:, cols(q)]
        mom_d[rows(q), :] = mom_v[:, cols(q)]

    def add(k, acc):
        source = rep_at(n - offset(k))
        remote(send_v.at[source], recv_v.at[source], rs_send.at[source], rs_recv.at[source], source, grp).wait_recv()
        return acc + recv_v[source].astype(f32)

    acc = send_v[me].astype(f32)
    if n <= 64:
        for k in range(n - 1):
            acc = add(k, acc)
    else:
        acc = lax.fori_loop(0, n - 1, add, acc)

    grad = snap_own[lane].astype(f32) - acc * (1.0 / n)
    g2 = grad * grad
    lanes = g2[:, 0:128]
    for k in range(1, part // 128):
        lanes = lanes + g2[:, k * 128:(k + 1) * 128]
    mine = grp * n + me
    sq[mine] = jnp.sum(lanes, axis=0, keepdims=True)

    def share(r, g):
        slot = g * n + r
        return remote(sq.at[mine], sq.at[mine], sq_send.at[slot], sq_recv.at[mine], r, g)

    def shared(r, g):
        slot = g * n + r
        return remote(sq.at[slot], sq.at[slot], sq_send.at[slot], sq_recv.at[slot], r, g)

    peers(lambda r, g: share(r, g).start())

    base = master_d[...]
    velocity = nesterov_mu * mom_d[...]
    peers(lambda r, g: shared(r, g).wait_recv())

    squares = jnp.sum(jnp.sum(sq[...], axis=0), axis=1, keepdims=True)
    grad_rms = jnp.sqrt(squares / elements + epsilon)
    scale = jnp.minimum(1.0, clip_limit / grad_rms)
    clipped = scale * grad
    new_momentum = velocity + clipped
    new_master = base - outer_rate * (clipped + nesterov_mu * new_momentum)
    gather_v[me] = new_master.astype(bf16)

    twin_row = plane * 4 + (1 - row) * 2 + core
    twin_core = plane * 4 + row * 2 + 1 - core

    def move(block, target, slot):
        return remote(gather_v.at[block], gather_v.at[block], ag_send.at[slot], ag_recv.at[block], target, grp)

    def place(i):
        return lax.rem(plane + i, planes)

    def block_of(i, r, c):
        return place(i) * 4 + r * 2 + c

    def unfold(i, r, c):
        where = place(i)
        for j in range(4):
            @pl.when(r * 2 + c == j)
            def _():
                for q in range(fold):
                    params_out[where, rows(j), cols(q)] = gather_v[where * 4 + j, rows(q), :]

    for i in range(1, planes):
        move(me, block_of(i, row, core), i).start()
    move(me, twin_row, planes).start()
    move(me, twin_core, 2 * planes).start()
    for q in range(fold):
        master_out[0, :, cols(q)] = new_master[rows(q), :]
        mom_out[0, :, cols(q)] = new_momentum[rows(q), :]
    unfold(0, row, core)
    for i in range(1, planes):
        block = block_of(i, row, core)
        move(block, block, 0).wait_recv()
        move(block, twin_row, planes + i).start()
        move(block, twin_core, 2 * planes + i).start()
        unfold(i, row, core)
    for i in range(planes):
        block = block_of(i, 1 - row, core)
        move(block, block, 0).wait_recv()
        move(block, twin_core, 3 * planes + i).start()
        unfold(i, 1 - row, core)
    for i in range(planes):
        for r in (row, 1 - row):
            block = block_of(i, r, 1 - core)
            move(block, block, 0).wait_recv()
            unfold(i, r, 1 - core)

    def drained(k):
        target = rep_at(1 + k)
        remote(send_v.at[target], recv_v.at[me], rs_send.at[target], rs_recv.at[me], target, grp).wait_send()
        move(me, twin_core, 1 + k).wait_send()

    each(n - 1, drained)
    peers(lambda r, g: share(r, g).wait_send())


def store(master_in, mom_in, params_in, master_out, mom_out, params_out, sem):
    copies = [
        pltpu.make_async_copy(params_in, params_out, sem.at[0]),
        pltpu.make_async_copy(master_in, master_out, sem.at[1]),
        pltpu.make_async_copy(mom_in, mom_out, sem.at[2]),
    ]
    for c in copies:
        c.start()
    for c in copies:
        c.wait()


def solution(mesh):
    n, groups = mesh.shape["rep"], mesh.shape["grp"]

    def body(local_params, snapshot, master, momentum):
        own, width = master.shape[1], master.shape[2]
        planes = n // 4
        span = 4 * own
        fold = max(1, 16 // own)
        deep, part = own * fold, width // fold
        hbm_spec = pl.BlockSpec(memory_space=pltpu.HBM)
        vmem_spec = pl.BlockSpec(memory_space=pltpu.VMEM)
        results = pl.pallas_call(
            functools.partial(kernel, n, groups, own, fold, snapshot.shape[1] * width * groups),
            out_shape=(
                pltpu.VMEM(master.shape, f32),
                pltpu.VMEM(master.shape, f32),
                pltpu.VMEM((planes, span, width), bf16),
            ),
            in_specs=[hbm_spec] * 4,
            out_specs=(vmem_spec,) * 3,
            scratch_shapes=[
                pltpu.VMEM((planes, span, width), bf16),
                pltpu.VMEM((span, width), bf16),
                pltpu.VMEM((own, width), f32),
                pltpu.VMEM((own, width), f32),
                pltpu.VMEM((n, deep, part), bf16),
                pltpu.VMEM((4, deep, part), bf16),
                pltpu.VMEM((deep, part), f32),
                pltpu.VMEM((deep, part), f32),
                pltpu.VMEM((n, deep, part), bf16),
                pltpu.VMEM((n, deep, part), bf16),
                pltpu.VMEM((n * groups, 1, 128), f32),
                pltpu.SemaphoreType.DMA((planes + 3,)),
                pltpu.SemaphoreType.DMA((n,)),
                pltpu.SemaphoreType.DMA((n,)),
                pltpu.SemaphoreType.DMA((n * groups,)),
                pltpu.SemaphoreType.DMA((n * groups,)),
                pltpu.SemaphoreType.DMA((n,)),
                pltpu.SemaphoreType.DMA((n,)),
            ],
            compiler_params=pltpu.CompilerParams(
                collective_id=0, has_side_effects=True, vmem_limit_bytes=32 * 2**20
            ),
        )(
            local_params.reshape(planes, span, width),
            snapshot.reshape(planes, span, width),
            master,
            momentum,
        )
        new_master, new_momentum, new_params = pl.pallas_call(
            store,
            out_shape=(
                jax.ShapeDtypeStruct(master.shape, f32),
                jax.ShapeDtypeStruct(master.shape, f32),
                jax.ShapeDtypeStruct((planes, span, width), bf16),
            ),
            in_specs=[vmem_spec] * 3,
            out_specs=(hbm_spec,) * 3,
            scratch_shapes=[pltpu.SemaphoreType.DMA((3,))],
            compiler_params=pltpu.CompilerParams(vmem_limit_bytes=16 * 2**20),
        )(*results)
        return new_master, new_momentum, new_params.reshape(snapshot.shape)

    return jax.shard_map(
        body,
        mesh=mesh,
        in_specs=(
            P("rep", "grp", None, None),
            P("grp", None, None),
            P("grp", "rep", None),
            P("grp", "rep", None),
        ),
        out_specs=(P("grp", "rep", None), P("grp", "rep", None), P("grp", None, None)),
        check_vma=False,
    )
```

time: 39.7 us -> 39.1 us (0.985)
    unnamed x5 -> x8, local copies, waits for them, and re-layouts: 4.01 us -> 3.75 us
    pallas_call x1 -> x2, Pallas kernels: 34.6 us -> 34.4 us  [the longest x1 33.6 us: body(): pl.pallas_call(functools.partial(kernel, n, groups, own, fold, snapshot.s...]
where the time goes in v2:
time: 39.1 us; the launch traced here: 38.8 us
  Pallas kernels  34.4 us (88%)
  local copies, waits for them, and re-layouts  3.75 us (10%)
  between operations  0.65 us (2%)
    pallas_call x1, Pallas kernels, body(): pl.pallas_call(functools.partial(kernel, n, groups, own, fold, snapshot.s...  33.6 us
    unnamed x8, local copies, waits for them, and re-layouts  3.75 us
    pallas_call x1, Pallas kernels, body(): pl.pallas_call(store, out_shape=(jax.ShapeDtypeStruct(master.shape, f32),...  0.85 us

profile of v2, /device:TPU:0, one launch (start us, length us, event | category | flops | bytes accessed | tf_op | source)
XLA Modules:
  0.0 38.8 jit_solution(3161672798500833528)
XLA Ops:
  0.6 0.0 copy-start
  0.6 1.0 %copy-done = bf16[1,1,32,8192]{3,2,1,0:T(8,128)(2,1)S(1)} copy-done((bf16[1,1,32,8192]{3,2,1,0:T(8,128)(2,1)S(1)}, bf16[1,1,32,8192]{3,2,1,0:T(8,128)(2,1)}, u32[]{:S(2)}) %copy-start) | copy-done | bytes 524312
  1.7 0.0 copy-start.1
  1.7 1.0 %copy-done.1 = bf16[1,32,8192]{2,1,0:T(8,128)(2,1)S(1)} copy-done((bf16[1,32,8192]{2,1,0:T(8,128)(2,1)S(1)}, bf16[1,32,8192]{2,1,0:T(8,128)(2,1)}, u32[]{:S(2)}) %copy-start.1) | copy-done | bytes 524312
  2.7 0.0 copy-start.2
  2.7 0.8 %copy-done.2 = f32[1,2,8192]{2,1,0:T(2,128)S(1)} copy-done((f32[1,2,8192]{2,1,0:T(2,128)S(1)}, f32[1,2,8192]{2,1,0:T(2,128)}, u32[]{:S(2)}) %copy-start.2) | copy-done | bytes 65560
  3.6 0.0 copy-start.3
  3.6 0.8 %copy-done.3 = f32[1,2,8192]{2,1,0:T(2,128)S(1)} copy-done((f32[1,2,8192]{2,1,0:T(2,128)S(1)}, f32[1,2,8192]{2,1,0:T(2,128)}, u32[]{:S(2)}) %copy-start.3) | copy-done | bytes 65560
  4.4 33.6 %shard_map.67 = (f32[1,2,8192]{2,1,0:T(2,128)S(1)}, f32[1,2,8192]{2,1,0:T(2,128)S(1)}, bf16[4,8,8192]{2,1,0:T(8,128)(2,1)S(1)}) custom-call(bf16[4,8,8192]{2,1,0:T(8,128)(2,1)S(1)} %bitcast.3, bf16[4,8,8192]{2,1,0:T(8,128)(2,1)S(1)} %bitcast.4, f32[1,2,8192]{2,1,0:T(2,128)S(1)} %copy-done.2, f32[1,2,8192]{2,1,0:T(2,128)S(1)} %copy-done.3), custom_call_target="tpu_custom_call" | custom-call | tf_op jit(solution)/shard_map/pallas_call | solution.py:230
  38.0 0.9 %shard_map.68 = (f32[1,2,8192]{2,1,0:T(2,128)}, f32[1,2,8192]{2,1,0:T(2,128)}, bf16[4,8,8192]{2,1,0:T(8,128)(2,1)}) custom-call(f32[1,2,8192]{2,1,0:T(2,128)S(1)} %get-tuple-element.9.master_in, f32[1,2,8192]{2,1,0:T(2,128)S(1)} %get-tuple-element.10.mom_in, bf16[4,8,8192]{2,1,0:T(8,128)(2,1)S(1)} %get-tuple-element.11.params_in), custom_call_target="tpu_custom_call" | custom-call | tf_op jit(solution)/shard_map/pallas_call | solution.py:268
Async XLA Ops:
  0.6 1.0 %copy-start = (bf16[1,1,32,8192]{3,2,1,0:T(8,128)(2,1)S(1)}, bf16[1,1,32,8192]{3,2,1,0:T(8,128)(2,1)}, u32[]{:S(2)}) copy-start(bf16[1,1,32,8192]{3,2,1,0:T(8,128)(2,1)} %param.4) | copy-start | bytes 1572868
  1.7 1.0 %copy-start.1 = (bf16[1,32,8192]{2,1,0:T(8,128)(2,1)S(1)}, bf16[1,32,8192]{2,1,0:T(8,128)(2,1)}, u32[]{:S(2)}) copy-start(bf16[1,32,8192]{2,1,0:T(8,128)(2,1)} %param.5) | copy-start | bytes 1572868
  2.7 0.8 %copy-start.2 = (f32[1,2,8192]{2,1,0:T(2,128)S(1)}, f32[1,2,8192]{2,1,0:T(2,128)}, u32[]{:S(2)}) copy-start(f32[1,2,8192]{2,1,0:T(2,128)} %master_hbm.1) | copy-start | bytes 196612
  3.6 0.8 %copy-start.3 = (f32[1,2,8192]{2,1,0:T(2,128)S(1)}, f32[1,2,8192]{2,1,0:T(2,128)}, u32[]{:S(2)}) copy-start(f32[1,2,8192]{2,1,0:T(2,128)} %mom_hbm.1) | copy-start | bytes 196612

commit v3 on v2

--- a/solution.py
+++ b/solution.py
@@ -225,6 +225,8 @@
         span = 4 * own
         fold = max(1, 16 // own)
         deep, part = own * fold, width // fold
+        results_size = (2 * snapshot.shape[1] + 8 * own) * width
+        grant = min(60 * 1024 * 2**10, 63 * 2**20 - results_size)
         hbm_spec = pl.BlockSpec(memory_space=pltpu.HBM)
         vmem_spec = pl.BlockSpec(memory_space=pltpu.VMEM)
         results = pl.pallas_call(
@@ -257,7 +259,7 @@
                 pltpu.SemaphoreType.DMA((n,)),
             ],
             compiler_params=pltpu.CompilerParams(
-                collective_id=0, has_side_effects=True, vmem_limit_bytes=32 * 2**20
+                collective_id=0, has_side_effects=True, vmem_limit_bytes=grant
             ),
         )(
             local_params.reshape(planes, span, width),

time: 39.1 us -> 34.3 us (0.88)
  local copies, waits for them, and re-layouts: 3.75 us -> 0 us
  Pallas kernels: 34.4 us -> 33.5 us
    unnamed x8 -> x0, local copies, waits for them, and re-layouts: 3.75 us -> none
    pallas_call x1, Pallas kernels: 33.6 us -> 32.6 us  [body(): pl.pallas_call(functools.partial(kernel, n, groups, own, fold, snapshot.s...]
where the time goes in v3:
time: 34.3 us; the launch traced here: 34.1 us
  Pallas kernels  33.5 us (98%)
  between operations  0.64 us (2%)
    pallas_call x1, Pallas kernels, body(): pl.pallas_call(functools.partial(kernel, n, groups, own, fold, snapshot.s...  32.6 us
    pallas_call x1, Pallas kernels, body(): pl.pallas_call(store, out_shape=(jax.ShapeDtypeStruct(master.shape, f32),...  0.85 us

profile of v3, /device:TPU:0, one launch (start us, length us, event | category | flops | bytes accessed | tf_op | source)
XLA Modules:
  0.0 34.1 jit_solution(9272933611287931791)
XLA Ops:
  0.6 32.6 %shard_map.67 = (f32[1,2,8192]{2,1,0:T(2,128)S(1)}, f32[1,2,8192]{2,1,0:T(2,128)S(1)}, bf16[4,8,8192]{2,1,0:T(8,128)(2,1)S(1)}) custom-call(bf16[4,8,8192]{2,1,0:T(8,128)(2,1)} %bitcast.3, bf16[4,8,8192]{2,1,0:T(8,128)(2,1)} %bitcast.4, f32[1,2,8192]{2,1,0:T(2,128)} %master_hbm.1, f32[1,2,8192]{2,1,0:T(2,128)} %mom_hbm.1), custom_call_target="tpu_custom_call" | custom-call | tf_op jit(solution)/shard_map/pallas_call | solution.py:232
  33.3 0.9 %shard_map.68 = (f32[1,2,8192]{2,1,0:T(2,128)}, f32[1,2,8192]{2,1,0:T(2,128)}, bf16[4,8,8192]{2,1,0:T(8,128)(2,1)}) custom-call(f32[1,2,8192]{2,1,0:T(2,128)S(1)} %get-tuple-element.9.master_in, f32[1,2,8192]{2,1,0:T(2,128)S(1)} %get-tuple-element.10.mom_in, bf16[4,8,8192]{2,1,0:T(8,128)(2,1)S(1)} %get-tuple-element.11.params_in), custom_call_target="tpu_custom_call" | custom-call | tf_op jit(solution)/shard_map/pallas_call | solution.py:270

commit v4 on v3

--- a/solution.py
+++ b/solution.py
@@ -38,8 +38,8 @@
     n, groups, own, fold, elements,
     local_hbm, snap_hbm, master_hbm, mom_hbm,
     master_out, mom_out, params_out,
-    local_v, snap_v, master_v, mom_v, send_v, snap_own, master_d, mom_d, recv_v, gather_v, sq,
-    in_sem, rs_send, rs_recv, sq_send, sq_recv, ag_send, ag_recv,
+    local_v, snap_v, master_v, mom_v, send_v, snap_own, master_d, mom_d, recv_v, part_v, sum_v, far_v, gather_v, sq,
+    in_sem, ready, part_send, part_recv, far_send, far_recv, rs_send, rs_recv, sq_send, sq_recv, ag_send, ag_recv,
 ):
     me = lax.axis_index("rep")
     grp = lax.axis_index("grp")
@@ -74,7 +74,13 @@
             each(n - 1, lambda i, g=g: body(rep_at(n - 1 - i), grp_at(g)))
 
     barrier = pltpu.get_barrier_semaphore()
-    peers(lambda r, g: pl.semaphore_signal(barrier, inc=1, device_id={"rep": r, "grp": g}, device_id_type=MESH))
+
+    def greet(semaphore, r, g):
+        pl.semaphore_signal(semaphore, inc=1, device_id={"rep": r, "grp": g}, device_id_type=MESH)
+
+    each(n - 1, lambda i: greet(barrier, rep_at(n - 1 - i), grp))
+    for g in range(1, groups):
+        greet(barrier, me, grp_at(g))
 
     def rows(q):
         return slice(q * own, (q + 1) * own)
@@ -88,16 +94,48 @@
             for q in range(fold):
                 send_v[p * 4 + j, rows(q), :] = local_v[p, rows(j), cols(q)]
 
-    pl.semaphore_wait(barrier, total - 1)
-
-    def offset(k):
-        return n // 2 + (1 - 2 * (k % 2)) * ((k + 1) // 2)
-
-    def scatter(k):
-        target = rep_at(offset(k))
-        remote(send_v.at[target], recv_v.at[me], rs_send.at[target], rs_recv.at[me], target, grp).start()
-
-    each(n - 1, scatter)
+    pl.semaphore_wait(barrier, n - 1 + groups - 1)
+    for g in range(1, groups):
+        greet(ready, me, grp_at(g))
+
+    def place(i):
+        return lax.rem(plane + i, planes)
+
+    def lane_at(d):
+        return lax.rem(lane + d, 4)
+
+    def collect(i, d):
+        to = lane_at(d)
+        return remote(send_v.at[place(i) * 4 + to], part_v.at[i, lane], part_send.at[i, to], part_recv.at[i, lane], plane * 4 + to, grp)
+
+    def collected(i, d):
+        source = lane_at(4 - d)
+        return remote(send_v.at[0], part_v.at[i, source], part_send.at[i, source], part_recv.at[i, source], plane * 4 + source, grp)
+
+    def forward(i):
+        return remote(sum_v.at[i], far_v.at[i], far_send.at[i], far_recv.at[i], place(i) * 4 + lane, grp)
+
+    def scatter(i, d):
+        target = place(i) * 4 + lane_at(d)
+        return remote(send_v.at[target], recv_v.at[i, lane], rs_send.at[i, lane_at(d)], rs_recv.at[i, lane], target, grp)
+
+    def scattered(i, d):
+        source = lane_at(4 - d)
+        return remote(send_v.at[0], recv_v.at[i, source], rs_send.at[i, source], rs_recv.at[i, source], place(planes - i) * 4 + source, grp)
+
+    direct = [(i, d) for i in (1, 0) for d in range(4) if i or d]
+    for i in range(2, planes):
+        for d in (1, 2, 3):
+            collect(i, d).start()
+    for i, d in direct:
+        scatter(i, d).start()
+    for i in range(2, planes):
+        both = send_v[place(i) * 4 + lane].astype(f32)
+        for d in (1, 2, 3):
+            collected(i, d).wait_recv()
+            both = both + part_v[i, lane_at(4 - d)].astype(f32)
+        sum_v[i] = both
+        forward(i).start()
 
     snap_load.wait()
     master_load.wait()
@@ -108,17 +146,13 @@
         master_d[rows(q), :] = master_v[:, cols(q)]
         mom_d[rows(q), :] = mom_v[:, cols(q)]
 
-    def add(k, acc):
-        source = rep_at(n - offset(k))
-        remote(send_v.at[source], recv_v.at[source], rs_send.at[source], rs_recv.at[source], source, grp).wait_recv()
-        return acc + recv_v[source].astype(f32)
-
     acc = send_v[me].astype(f32)
-    if n <= 64:
-        for k in range(n - 1):
-            acc = add(k, acc)
-    else:
-        acc = lax.fori_loop(0, n - 1, add, acc)
+    for i, d in reversed(direct):
+        scattered(i, d).wait_recv()
+        acc = acc + recv_v[i, lane_at(4 - d)].astype(f32)
+    for i in range(2, planes):
+        forward(i).wait_recv()
+        acc = acc + far_v[i]
 
     grad = snap_own[lane].astype(f32) - acc * (1.0 / n)
     g2 = grad * grad
@@ -136,6 +170,7 @@
         slot = g * n + r
         return remote(sq.at[slot], sq.at[slot], sq_send.at[slot], sq_recv.at[slot], r, g)
 
+    pl.semaphore_wait(ready, groups - 1)
     peers(lambda r, g: share(r, g).start())
 
     base = master_d[...]
@@ -155,9 +190,6 @@
 
     def move(block, target, slot):
         return remote(gather_v.at[block], gather_v.at[block], ag_send.at[slot], ag_recv.at[block], target, grp)
-
-    def place(i):
-        return lax.rem(plane + i, planes)
 
     def block_of(i, r, c):
         return place(i) * 4 + r * 2 + c
@@ -195,9 +227,14 @@
             move(block, block, 0).wait_recv()
             unfold(i, r, 1 - core)
 
+    for i in range(2, planes):
+        for d in (1, 2, 3):
+            collect(i, d).wait_send()
+        forward(i).wait_send()
+    for i, d in direct:
+        scatter(i, d).wait_send()
+
     def drained(k):
-        target = rep_at(1 + k)
-        remote(send_v.at[target], recv_v.at[me], rs_send.at[target], rs_recv.at[me], target, grp).wait_send()
         move(me, twin_core, 1 + k).wait_send()
 
     each(n - 1, drained)
@@ -247,12 +284,20 @@
                 pltpu.VMEM((4, deep, part), bf16),
                 pltpu.VMEM((deep, part), f32),
                 pltpu.VMEM((deep, part), f32),
-                pltpu.VMEM((n, deep, part), bf16),
+                pltpu.VMEM((2, 4, deep, part), bf16),
+                pltpu.VMEM((planes, 4, deep, part), bf16),
+                pltpu.VMEM((planes, deep, part), f32),
+                pltpu.VMEM((planes, deep, part), f32),
                 pltpu.VMEM((n, deep, part), bf16),
                 pltpu.VMEM((n * groups, 1, 128), f32),
                 pltpu.SemaphoreType.DMA((planes + 3,)),
-                pltpu.SemaphoreType.DMA((n,)),
-                pltpu.SemaphoreType.DMA((n,)),
+                pltpu.SemaphoreType.REGULAR,
+                pltpu.SemaphoreType.DMA((planes, 4)),
+                pltpu.SemaphoreType.DMA((planes, 4)),
+                pltpu.SemaphoreType.DMA((planes,)),
+                pltpu.SemaphoreType.DMA((planes,)),
+                pltpu.SemaphoreType.DMA((2, 4)),
+                pltpu.SemaphoreType.DMA((2, 4)),
                 pltpu.SemaphoreType.DMA((n * groups,)),
                 pltpu.SemaphoreType.DMA((n * groups,)),
                 pltpu.SemaphoreType.DMA((n,)),

time: 34.3 us -> 32.5 us (0.948)
  Pallas kernels: 33.5 us -> 31.7 us
    pallas_call x1, Pallas kernels: 32.6 us -> 30.8 us  [body(): pl.pallas_call(functools.partial(kernel, n, groups, own, fold, snapshot.s...]
where the time goes in v4:
time: 32.5 us; the launch traced here: 32.3 us
  Pallas kernels  31.7 us (98%)
  between operations  0.64 us (2%)
    pallas_call x1, Pallas kernels, body(): pl.pallas_call(functools.partial(kernel, n, groups, own, fold, snapshot.s...  30.8 us
    pallas_call x1, Pallas kernels, body(): pl.pallas_call(store, out_shape=(jax.ShapeDtypeStruct(master.shape, f32),...  0.85 us

profile of v4, /device:TPU:0, one launch (start us, length us, event | category | flops | bytes accessed | tf_op | source)
XLA Modules:
  0.0 32.3 jit_solution(2546770311682598508)
XLA Ops:
  0.6 30.8 %shard_map.67 = (f32[1,2,8192]{2,1,0:T(2,128)S(1)}, f32[1,2,8192]{2,1,0:T(2,128)S(1)}, bf16[4,8,8192]{2,1,0:T(8,128)(2,1)S(1)}) custom-call(bf16[4,8,8192]{2,1,0:T(8,128)(2,1)} %bitcast.3, bf16[4,8,8192]{2,1,0:T(8,128)(2,1)} %bitcast.4, f32[1,2,8192]{2,1,0:T(2,128)} %master_hbm.1, f32[1,2,8192]{2,1,0:T(2,128)} %mom_hbm.1), custom_call_target="tpu_custom_call" | custom-call | tf_op jit(solution)/shard_map/pallas_call | solution.py:269
  31.5 0.9 %shard_map.68 = (f32[1,2,8192]{2,1,0:T(2,128)}, f32[1,2,8192]{2,1,0:T(2,128)}, bf16[4,8,8192]{2,1,0:T(8,128)(2,1)}) custom-call(f32[1,2,8192]{2,1,0:T(2,128)S(1)} %get-tuple-element.9.master_in, f32[1,2,8192]{2,1,0:T(2,128)S(1)} %get-tuple-element.10.mom_in, bf16[4,8,8192]{2,1,0:T(8,128)(2,1)S(1)} %get-tuple-element.11.params_in), custom_call_target="tpu_custom_call" | custom-call | tf_op jit(solution)/shard_map/pallas_call | solution.py:315
